TPU v7x, 32 devices: a whole 2x2x4 slice. The times are simulated.
32 devices in a mesh: gx: 4 (over y, x), gy: 4 (over z), row: 2 (over core).
Axes of the slice: x: 2, y: 2, z: 4, core: 2. Of those that a mesh axis runs over, the one named last changes fastest.
Arguments:
- columns: bfloat16 [137, 131072], P(None, ('gx', 'gy')), may hold values from -6 to 6
- level_weights: bfloat16 [137, 16], replicated, may hold values from -0.5 to 0.5
- orbit_term: float32 [16, 32], replicated, may hold values from -6 to 6
- col_owner: int32 [524288, 1], P(('gx', 'gy', 'row')), may hold values from 0 to 15; in each aligned block of 16384 rows (0 to 16383, 16384 to 32767, ...) at most 2048 rows name the same one
- col_local: int32 [524288], P(('gx', 'gy', 'row')), may hold values from 0 to 8191
- orbit_bin: int32 [524288], P(('gx', 'gy', 'row')), may hold values from 0 to 31
- group_id: int32 [524288], P(('gx', 'gy', 'row')), may hold values from 0 to 63
- departure: float32 [524288], P(('gx', 'gy', 'row')), may hold values from -6 to 6
Outputs:
- covariance: float32 [16, 16, 64], P(None, None, 'row')
- cross: float32 [16, 64], P(None, 'row')
Inputs may be any that keep to these rules, and one draw needn't show every extreme that they name: `col_owner`: among the footprints of one device, no owning device is named more than 2048 times; some owning device is named exactly 2048 times.
All inputs are finite; a program needn't handle non-finite values.
Results may differ from a plain program's by a relative error of at most 0.0022.
Values may be sent and summed in bfloat16 or wider, within the bound.
A program may use at most 128 MiB of HBM per device.

v0:
```python
import math
import jax
import jax.numpy as jnp
from jax import lax
from jax.sharding import PartitionSpec as P

NGRP = 64


def send_request(wanted):
    return lax.all_to_all(wanted, ("gx", "gy"), split_axis=0, concat_axis=0, tiled=True)


def send_answer(picked):
    return lax.all_to_all(picked, ("gx", "gy"), split_axis=1, concat_axis=1, tiled=True)


def local(columns, level_weights, orbit_term, col_owner, col_local, orbit_bin, group_id, departure):
    grid_x = lax.axis_size("gx")
    grid_y = lax.axis_size("gy")
    owners = grid_x * grid_y
    footprints = col_owner.shape[0]
    capacity = 2 * footprints // owners
    slots_all = owners * capacity
    npred = level_weights.shape[1]
    ngroups = NGRP
    owner = col_owner[:, 0]
    owner_hits = (owner[:, None] == jnp.arange(owners, dtype=jnp.int32)[None, :]).astype(jnp.int32)
    ranks = jnp.cumsum(owner_hits, axis=0)
    slot = jnp.sum(ranks * owner_hits, axis=1) - 1
    target = owner * capacity + slot
    stacked = jnp.stack([col_local, orbit_bin, group_id], axis=0)
    placed = jnp.full((3, slots_all), -1, jnp.int32).at[:, target].set(stacked)
    slot_depart = jnp.zeros((slots_all,), jnp.float32).at[target].set(departure)
    wanted = jnp.maximum(placed[0], 0).reshape(owners, capacity)
    asked = send_request(wanted)
    thickness = jnp.dot(level_weights.T, columns, preferred_element_type=jnp.float32).astype(
        jnp.bfloat16
    )
    picked = thickness[:, asked]
    back = send_answer(picked)
    flat = back.reshape(npred, slots_all)
    slot_bin = placed[1]
    slot_group = placed[2]
    width = math.gcd(slots_all, 4096)
    nblocks = slots_all // width
    bin_range = jnp.arange(orbit_term.shape[1], dtype=jnp.int32)
    group_range = jnp.arange(ngroups, dtype=jnp.int32)

    def accumulate(carry, which):
        prod_acc, sum_acc, count_acc = carry
        first = which * width
        part_flat = lax.dynamic_slice_in_dim(flat, first, width, 1)
        part_bin = lax.dynamic_slice_in_dim(slot_bin, first, width, 0)
        grp = lax.dynamic_slice_in_dim(slot_group, first, width, 0)
        dep = lax.dynamic_slice_in_dim(slot_depart, first, width, 0)
        bin_hits = (bin_range[:, None] == part_bin[None, :]).astype(jnp.float32)
        block = part_flat.astype(jnp.float32) + jnp.dot(
            orbit_term,
            bin_hits,
            precision=lax.Precision.HIGHEST,
            preferred_element_type=jnp.float32,
        )
        hits = (grp[:, None] == group_range[None, :]).astype(jnp.float32)
        outer = (block[:, None, :] * block[None, :, :]).reshape(npred * npred, width)
        prod_acc = prod_acc + jnp.dot(
            outer, hits, precision=lax.Precision.HIGHEST, preferred_element_type=jnp.float32
        )
        sum_acc = sum_acc + jnp.dot(
            block * dep[None, :],
            hits,
            precision=lax.Precision.HIGHEST,
            preferred_element_type=jnp.float32,
        )
        count_acc = count_acc + jnp.sum(hits, axis=0)[None, :]
        return ((prod_acc, sum_acc, count_acc), None)

    start = (
        jnp.zeros((npred * npred, ngroups), jnp.float32),
        jnp.zeros((npred, ngroups), jnp.float32),
        jnp.zeros((1, ngroups), jnp.float32),
    )
    (products, sums, count), _ = lax.scan(accumulate, start, jnp.arange(nblocks, dtype=jnp.int32))
    share = ngroups // lax.axis_size("row")
    products, sums, count = (
        lax.psum_scatter(products, "row", scatter_dimension=1, tiled=True),
        lax.psum_scatter(sums, "row", scatter_dimension=1, tiled=True),
        lax.psum_scatter(count, "row", scatter_dimension=1, tiled=True),
    )
    products, sums, count = lax.psum((products, sums, count), ("gx", "gy"))
    scale = 1.0 / (count + 1.0)
    covariance = (products * scale).reshape(npred, npred, share)
    cross = sums * scale
    return (covariance, cross)


def solution(mesh):
    in_specs = (
        P(None, ("gx", "gy")),
        P(),
        P(),
        P(("gx", "gy", "row"), None),
        P(("gx", "gy", "row")),
        P(("gx", "gy", "row")),
        P(("gx", "gy", "row")),
        P(("gx", "gy", "row")),
    )
    out_specs = (P(None, None, "row"), P(None, "row"))
    return jax.shard_map(local, mesh=mesh, in_specs=in_specs, out_specs=out_specs, check_vma=False)
```

profile of v0, /device:TPU:0, one launch (start us, length us, event | category | flops | bytes accessed | tf_op | source)
XLA Modules:
  0.0 520.1 jit_solution(6604722221456737863)
XLA Ops:
  7.2 1.1 copy.35
  8.7 1.1 broadcast_add_fusion
  9.8 1.6 copy.36
  11.4 1.6 fusion.17
  13.0 0.9 compare_select_fusion.1
  14.0 1.1 add_bitcast_fusion
  15.1 5.1 copy.37
  20.1 47.4 %scatter_custom_fusion = s32[3,32768]{0,1:T(8,128)} fusion(s32[16384]{0:T(1024)S(1)} %bitcast.78, s32[16384,3]{1,0:T(8,128)} %copy.37, s32[]{:T(128)} %constant.6.clone.1), kind=kCustom, calls=%fused_computation.26 | custom fusion | bytes 393728 | tf_op jit(solution)/shard_map/scatter | solution.py:33
  67.5 30.9 %slice_reduce_fusion = (s32[32768]{0:T(1024)}, s32[32768]{0:T(1024)}, s32[32768]{0:T(1024)}) fusion(s32[3,32768]{0,1:T(8,128)} %scatter_custom_fusion), kind=kLoop, calls=%fused_computation.21 | loop fusion | flops 32768 | bytes 786432 | tf_op jit(solution)/shard_map/slice | solution.py:44
  98.4 8.3 %all-to-all-start = ((s32[16,1,2048]{2,1,0:T(1,128)}), s32[16,1,2048]{2,1,0:T(1,128)S(1)}, u32[]{:S(2)}, u32[]{:S(2)}) async-start(s32[16,1,2048]{2,1,0:T(1,128)} %bitcast.24), calls=%async_computation | async-start | bytes 262144 | tf_op jit(solution)/shard_map/all_to_all | solution.py:11
  107.2 1.8 copy.39
  109.0 5.5 %all-to-all-done = s32[16,1,2048]{2,1,0:T(1,128)S(1)} async-done(((s32[16,1,2048]{2,1,0:T(1,128)}), s32[16,1,2048]{2,1,0:T(1,128)S(1)}, u32[]{:S(2)}, u32[]{:S(2)}) %all-to-all-start) | async-done | bytes 131104 | tf_op jit(solution)/shard_map/all_to_all | solution.py:11
  114.6 111.2 %gather_fusion = bf16[32768,16]{1,0:T(8,128)(2,1)} fusion(bf16[16,8192]{0,1:T(8,128)(2,1)} %copy.39, s32[32768]{0:T(1024)S(1)} %broadcast_clamp_fusion), kind=kCustom, calls=%fused_computation | custom fusion | bytes 2228224 | tf_op jit(solution)/shard_map/gather | solution.py:40
  225.8 7.8 %copy.40 = bf16[16,2048,16]{1,2,0:T(8,128)(2,1)} copy(bf16[16,2048,16]{2,1,0:T(8,128)(2,1)} %bitcast.64) | data formatting | bytes 2097152 | tf_op jit(solution)/shard_map/gather | solution.py:40
  233.6 3.7 all-to-all-start.1
  237.4 61.1 %scatter_custom_fusion.1 = f32[32768]{0:T(1024)} fusion(s32[16384]{0:T(1024)S(1)} %bitcast.79, f32[16384]{0:T(1024)} %param.17, f32[]{:T(128)} %constant.20.clone.1), kind=kCustom, calls=%fused_computation.41 | custom fusion | bytes 131584 | tf_op jit(solution)/shard_map/scatter | solution.py:34
  298.5 1.0 copy.47
  299.6 103.2 %while.15 = (s32[]{:T(128)}, f32[256,64]{0,1:T(8,128)S(1)}, f32[16,64]{1,0:T(8,128)}, f32[1,64]{1,0:T(1,128)S(1)}, s32[8]{0:T(128)S(1)}, /*index=5*/bf16[16,3276...) while((s32[]{:T(128)}, f32[256,64]{0,1:T(8,128)S(1)}, ...), condition=%wide.region_7.8_spmd.clone, body=%wide.region_5.7_spmd.clone.sunk | while | flops 883525696 | bytes 9661715 | solution.py:83
  300.9 0.7 dynamic_slice.29
  301.6 1.2 fusion.36
  302.8 2.4 broadcast_multiply_fusion.4
  306.0 4.5 convolution_add_fusion.4
  310.5 0.7 dynamic_slice.31
  313.8 0.7 dynamic_slice.29
  314.5 1.2 fusion.36
  315.7 2.4 broadcast_multiply_fusion.4
  318.9 4.5 convolution_add_fusion.4
  323.4 0.7 dynamic_slice.31
  326.7 0.7 dynamic_slice.29
  327.4 1.2 fusion.36
  328.6 2.4 broadcast_multiply_fusion.4
  331.8 4.5 convolution_add_fusion.4
  336.3 0.7 dynamic_slice.31
  339.6 0.7 dynamic_slice.29
  340.3 1.2 fusion.36
  341.5 2.4 broadcast_multiply_fusion.4
  344.7 4.5 convolution_add_fusion.4
  349.2 0.7 dynamic_slice.31
  352.5 0.7 dynamic_slice.29
  353.2 1.2 fusion.36
  354.4 2.4 broadcast_multiply_fusion.4
  357.6 4.5 convolution_add_fusion.4
  362.1 0.7 dynamic_slice.31
  365.4 0.7 dynamic_slice.29
  366.1 1.2 fusion.36
  367.3 2.4 broadcast_multiply_fusion.4
  370.5 4.5 convolution_add_fusion.4
  375.0 0.7 dynamic_slice.31
  378.3 0.7 dynamic_slice.29
  379.0 1.2 fusion.36
  380.2 2.4 broadcast_multiply_fusion.4
  383.4 4.5 convolution_add_fusion.4
  387.9 0.7 dynamic_slice.31
  391.9 1.2 fusion.36
  393.1 2.4 broadcast_multiply_fusion.4
  396.3 4.5 convolution_add_fusion.4
  403.5 1.4 copy.45
  405.7 6.7 %reduce-scatter.10.cloned.1.call-done = f32[32,1]{1,0:T(8,128)} async-done(((f32[64,1]{1,0:T(8,128)}), f32[32,1]{1,0:T(8,128)}) %reduce-scatter.10.cloned.1.call-update) | async-done | bytes 144
  412.4 0.8 copy.44
  413.2 10.1 %reduce-scatter.12.cloned.1.call-done = f32[32,16]{1,0:T(8,128)} async-done(((f32[64,16]{1,0:T(8,128)}), f32[32,16]{1,0:T(8,128)}) %reduce-scatter.12.cloned.1.call-update) | async-done | bytes 2064
  423.3 0.8 copy.46
  424.1 10.7 %reduce-scatter.8.cloned.1.call-done = f32[256,32]{0,1:T(8,128)} async-done(((f32[256,64]{0,1:T(8,128)}), f32[256,32]{0,1:T(8,128)}) %reduce-scatter.8.cloned.1.call-update) | async-done | bytes 32784 | tf_op jit(solution)/shard_map/reduce_scatter | solution.py:86
  434.7 77.4 %all-reduce = (f32[256,32]{0,1:T(8,128)S(1)}, f32[1,32]{1,0:T(1,128)S(1)}, f32[16,32]{1,0:T(8,128)S(1)}) all-reduce(f32[256,32]{0,1:T(8,128)} %reduce-scatter.8.cloned.1.call-done, f32[1,32]{1,0:T(1,128)S(1)} %copy.44, f32[16,32]{1,0:T(8,128)S(1)} %copy.46), channel_id=1, replica_groups=mesh['gx'=4,'gy'=4,'row'=2] {'gx','gy'}, use_global_device_ids=true, to_apply=%region_9.10 | all-reduce | flops 8736 | bytes 69888 | tf_op jit(solution)/shard_map/psum | solution.py:90
  512.8 0.8 copy.42
  (105 shorter events, 25.6 us)
Async XLA Ops:
  7.2 99.6 %copy-start = (bf16[137,8192]{1,0:T(8,128)(2,1)S(1)}, bf16[137,8192]{1,0:T(8,128)(2,1)}, u32[]{:S(2)}) copy-start(bf16[137,8192]{1,0:T(8,128)(2,1)} %param.10) | copy-start | bytes 6733828
  67.5 39.3 %copy-start.3 = (bf16[137,16]{0,1:T(8,128)(2,1)S(1)}, bf16[137,16]{0,1:T(8,128)(2,1)}, u32[]{:S(2)}) copy-start(bf16[137,16]{0,1:T(8,128)(2,1)} %param.11) | copy-start | bytes 13156
  98.4 16.0 %all-to-all-start = ((s32[16,1,2048]{2,1,0:T(1,128)}), s32[16,1,2048]{2,1,0:T(1,128)S(1)}, u32[]{:S(2)}, u32[]{:S(2)}) async-start(s32[16,1,2048]{2,1,0:T(1,128)} %bitcast.24), calls=%async_computation | async-start | bytes 262144 | tf_op jit(solution)/shard_map/all_to_all | solution.py:11
  225.8 73.7 %copy-start.2 = (f32[16,32]{1,0:T(8,128)S(1)}, f32[16,32]{1,0:T(8,128)}, u32[]{:S(2)}) copy-start(f32[16,32]{1,0:T(8,128)} %param.12) | copy-start | bytes 6148
  233.6 64.9 %all-to-all-start.1 = ((bf16[16,16,2048]{2,0,1:T(8,128)(2,1)}), bf16[16,16,2048]{2,0,1:T(8,128)(2,1)S(1)}, u32[]{:S(2)}, u32[]{:S(2)}) async-start(bf16[16,16,2048]{2,0,1:T(8,128)(2,1)} %bitcast.13), calls=%async_computation.1 | async-start | bytes 2097152 | tf_op jit(solution)/shard_map/all_to_all | solution.py:15
  237.3 175.1 %reduce-scatter.10.cloned.1.call-start = ((), (), s32[]{:S(2)}) async-start(), calls=%async_computation.6 | async-start | bytes 49152
  299.6 11.7 %copy-start.4 = (f32[16,64]{1,0:T(8,128)S(1)}, f32[16,64]{1,0:T(8,128)}, u32[]{:S(2)}) copy-start(f32[16,64]{1,0:T(8,128)} %get-tuple-element.209) | copy-start | bytes 12292 | tf_op jit(solution)/shard_map/while
  311.8 0.6 copy-start.5
  312.5 11.7 %copy-start.4 = (f32[16,64]{1,0:T(8,128)S(1)}, f32[16,64]{1,0:T(8,128)}, u32[]{:S(2)}) copy-start(f32[16,64]{1,0:T(8,128)} %get-tuple-element.209) | copy-start | bytes 12292 | tf_op jit(solution)/shard_map/while
  324.7 0.6 copy-start.5
  325.4 11.7 %copy-start.4 = (f32[16,64]{1,0:T(8,128)S(1)}, f32[16,64]{1,0:T(8,128)}, u32[]{:S(2)}) copy-start(f32[16,64]{1,0:T(8,128)} %get-tuple-element.209) | copy-start | bytes 12292 | tf_op jit(solution)/shard_map/while
  337.6 0.6 copy-start.5
  338.2 11.7 %copy-start.4 = (f32[16,64]{1,0:T(8,128)S(1)}, f32[16,64]{1,0:T(8,128)}, u32[]{:S(2)}) copy-start(f32[16,64]{1,0:T(8,128)} %get-tuple-element.209) | copy-start | bytes 12292 | tf_op jit(solution)/shard_map/while
  350.5 0.6 copy-start.5
  351.1 11.7 %copy-start.4 = (f32[16,64]{1,0:T(8,128)S(1)}, f32[16,64]{1,0:T(8,128)}, u32[]{:S(2)}) copy-start(f32[16,64]{1,0:T(8,128)} %get-tuple-element.209) | copy-start | bytes 12292 | tf_op jit(solution)/shard_map/while
  363.4 0.6 copy-start.5
  364.1 11.7 %copy-start.4 = (f32[16,64]{1,0:T(8,128)S(1)}, f32[16,64]{1,0:T(8,128)}, u32[]{:S(2)}) copy-start(f32[16,64]{1,0:T(8,128)} %get-tuple-element.209) | copy-start | bytes 12292 | tf_op jit(solution)/shard_map/while
  376.3 0.6 copy-start.5
  376.9 11.7 %copy-start.4 = (f32[16,64]{1,0:T(8,128)S(1)}, f32[16,64]{1,0:T(8,128)}, u32[]{:S(2)}) copy-start(f32[16,64]{1,0:T(8,128)} %get-tuple-element.209) | copy-start | bytes 12292 | tf_op jit(solution)/shard_map/while
  389.2 0.6 copy-start.5
  389.8 11.7 %copy-start.4 = (f32[16,64]{1,0:T(8,128)S(1)}, f32[16,64]{1,0:T(8,128)}, u32[]{:S(2)}) copy-start(f32[16,64]{1,0:T(8,128)} %get-tuple-element.209) | copy-start | bytes 12292 | tf_op jit(solution)/shard_map/while
  402.1 0.6 copy-start.5
  402.7 2.2 copy-start.1
  403.5 19.8 %reduce-scatter.12.cloned.1.call-start = ((), (), s32[]{:S(2)}) async-start(), calls=%async_computation.7 | async-start | bytes 49152
  404.9 29.8 %reduce-scatter.8.cloned.1.call-start = ((), (), s32[]{:S(2)}) async-start(), calls=%async_computation.5 | async-start | bytes 98304 | tf_op jit(solution)/shard_map/reduce_scatter | solution.py:86
Sparse Core Ops, SparseCore 0:
  403.6 8.7 reduce-scatter.9
  414.6 8.6 reduce-scatter.11
  426.0 8.6 reduce-scatter.7
where the time goes:
time: 523 us; the launch traced here: 520 us
  local copies, waits for them, and re-layouts  268 us (51%)
  blocking collectives  77.4 us (15%)
  other arithmetic  57.9 us (11%)
  matrix products  51.1 us (10%)
  waiting for transfers between devices  33.7 us (6%)
  between operations  13.9 us (3%)
  starting transfers between devices  12.1 us (2%)
  loops' own time  5.87 us (1%)
    gather x2, local copies, waits for them, and re-layouts, local(): picked = thickness[:, asked]  119 us
    psum x1, blocking collectives, local(): products, sums, count = lax.psum((products, sums, count), ('gx', 'gy'))  77.4 us
    scatter x1, local copies, waits for them, and re-layouts, local(): slot_depart = jnp.zeros((slots_all,), jnp.float32).at[target].set(departure)  61.1 us
    scatter x1, local copies, waits for them, and re-layouts, local(): placed = jnp.full((3, slots_all), -1, jnp.int32).at[:, target].set(stacked)  47.4 us
    dot_general x8, matrix products, accumulate(): jnp.dot(outer, hits, precision=lax.Precision.HIGHEST, preferred_element_t...  36.2 us
    slice x1, other arithmetic, local(): slot_group = placed[2]  30.9 us
    mul x8, other arithmetic, accumulate(): block[:, None, :] * block[None, :, :]  19.2 us
    unnamed x5, waiting for transfers between devices  17.5 us
  transfers between devices with their start and end apart: 5, of which 4 were waited for; matrix products, arithmetic and copies ran while one was open for 13% of the time, Pallas kernels for 0%

commit v1 on v0

--- a/solution.py
+++ b/solution.py
@@ -5,6 +5,11 @@
 from jax.sharding import PartitionSpec as P
 
 NGRP = 64
+
+
+def axis_by_axis(value, one, other):
+    inner = lax.psum(value, one)
+    return lax.psum(inner, other)
 
 
 def send_request(wanted):
@@ -87,7 +92,7 @@
         lax.psum_scatter(sums, "row", scatter_dimension=1, tiled=True),
         lax.psum_scatter(count, "row", scatter_dimension=1, tiled=True),
     )
-    products, sums, count = lax.psum((products, sums, count), ("gx", "gy"))
+    products, sums, count = axis_by_axis((products, sums, count), "gy", "gx")
     scale = 1.0 / (count + 1.0)
     covariance = (products * scale).reshape(npred, npred, share)
     cross = sums * scale

time: 523 us -> 482 us (0.922)
  blocking collectives: 77.4 us -> 36.7 us
    psum x1 -> x2, blocking collectives: 77.4 us -> 36.7 us  [the longest x1 20.1 us: axis_by_axis(): inner = lax.psum(value, one)]
  transfers between devices with their start and end apart: 5 -> 5, of which waited for: 4 -> 4; matrix products, arithmetic and copies ran while one was open for 13% -> 14% of each run, Pallas kernels for 0% -> 0%
where the time goes in v1:
time: 482 us; the launch traced here: 479 us
  local copies, waits for them, and re-layouts  268 us (56%)
  other arithmetic  57.9 us (12%)
  matrix products  51.1 us (11%)
  blocking collectives  36.7 us (8%)
  waiting for transfers between devices  33.7 us (7%)
  between operations  13.9 us (3%)
  starting transfers between devices  12.1 us (3%)
  loops' own time  5.87 us (1%)
    gather x2, local copies, waits for them, and re-layouts, local(): picked = thickness[:, asked]  119 us
    scatter x1, local copies, waits for them, and re-layouts, local(): slot_depart = jnp.zeros((slots_all,), jnp.float32).at[target].set(departure)  61.1 us
    scatter x1, local copies, waits for them, and re-layouts, local(): placed = jnp.full((3, slots_all), -1, jnp.int32).at[:, target].set(stacked)  47.4 us
    dot_general x8, matrix products, accumulate(): jnp.dot(outer, hits, precision=lax.Precision.HIGHEST, preferred_element_t...  36.2 us
    slice x1, other arithmetic, local(): slot_group = placed[2]  30.9 us
    psum x1, blocking collectives, axis_by_axis(): inner = lax.psum(value, one)  20.1 us
    mul x8, other arithmetic, accumulate(): block[:, None, :] * block[None, :, :]  19.2 us
    unnamed x5, waiting for transfers between devices  17.5 us
  transfers between devices with their start and end apart: 5, of which 4 were waited for; matrix products, arithmetic and copies ran while one was open for 14% of the time, Pallas kernels for 0%

profile of v1, /device:TPU:0, one launch (start us, length us, event | category | flops | bytes accessed | tf_op | source)
XLA Modules:
  0.0 479.4 jit_solution(6794877788336958983)
XLA Ops:
  7.2 1.1 copy.35
  8.7 1.1 broadcast_add_fusion
  9.8 1.6 copy.36
  11.4 1.6 fusion.17
  13.0 0.9 compare_select_fusion.1
  14.0 1.1 add_bitcast_fusion
  15.1 5.1 %copy.37 = s32[16384,3]{1,0:T(8,128)} copy(s32[16384,3]{0,1:T(4,128)S(1)} %add_bitcast_fusion) | data formatting | bytes 393216 | tf_op jit(solution)/shard_map/stack | solution.py:37
  20.1 47.4 %scatter_custom_fusion = s32[3,32768]{0,1:T(8,128)} fusion(s32[16384]{0:T(1024)S(1)} %bitcast.78, s32[16384,3]{1,0:T(8,128)} %copy.37, s32[]{:T(128)} %constant.6.clone.1), kind=kCustom, calls=%fused_computation.26 | custom fusion | bytes 393728 | tf_op jit(solution)/shard_map/scatter | solution.py:38
  67.5 30.9 %slice_reduce_fusion = (s32[32768]{0:T(1024)}, s32[32768]{0:T(1024)}, s32[32768]{0:T(1024)}) fusion(s32[3,32768]{0,1:T(8,128)} %scatter_custom_fusion), kind=kLoop, calls=%fused_computation.21 | loop fusion | flops 32768 | bytes 786432 | tf_op jit(solution)/shard_map/slice | solution.py:49
  98.4 8.3 %all-to-all-start = ((s32[16,1,2048]{2,1,0:T(1,128)}), s32[16,1,2048]{2,1,0:T(1,128)S(1)}, u32[]{:S(2)}, u32[]{:S(2)}) async-start(s32[16,1,2048]{2,1,0:T(1,128)} %bitcast.24), calls=%async_computation | async-start | bytes 262144 | tf_op jit(solution)/shard_map/all_to_all | solution.py:16
  107.2 1.8 copy.39
  109.0 5.5 %all-to-all-done = s32[16,1,2048]{2,1,0:T(1,128)S(1)} async-done(((s32[16,1,2048]{2,1,0:T(1,128)}), s32[16,1,2048]{2,1,0:T(1,128)S(1)}, u32[]{:S(2)}, u32[]{:S(2)}) %all-to-all-start) | async-done | bytes 131104 | tf_op jit(solution)/shard_map/all_to_all | solution.py:16
  114.6 111.2 %gather_fusion = bf16[32768,16]{1,0:T(8,128)(2,1)} fusion(bf16[16,8192]{0,1:T(8,128)(2,1)} %copy.39, s32[32768]{0:T(1024)S(1)} %broadcast_clamp_fusion), kind=kCustom, calls=%fused_computation | custom fusion | bytes 2228224 | tf_op jit(solution)/shard_map/gather | solution.py:45
  225.8 7.8 %copy.40 = bf16[16,2048,16]{1,2,0:T(8,128)(2,1)} copy(bf16[16,2048,16]{2,1,0:T(8,128)(2,1)} %bitcast.64) | data formatting | bytes 2097152 | tf_op jit(solution)/shard_map/gather | solution.py:45
  233.6 3.7 all-to-all-start.1
  237.4 61.1 %scatter_custom_fusion.1 = f32[32768]{0:T(1024)} fusion(s32[16384]{0:T(1024)S(1)} %bitcast.79, f32[16384]{0:T(1024)} %param.17, f32[]{:T(128)} %constant.20.clone.1), kind=kCustom, calls=%fused_computation.41 | custom fusion | bytes 131584 | tf_op jit(solution)/shard_map/scatter | solution.py:39
  298.5 1.0 copy.47
  299.6 103.2 %while.15 = (s32[]{:T(128)}, f32[256,64]{0,1:T(8,128)S(1)}, f32[16,64]{1,0:T(8,128)}, f32[1,64]{1,0:T(1,128)S(1)}, s32[8]{0:T(128)S(1)}, /*index=5*/bf16[16,3276...) while((s32[]{:T(128)}, f32[256,64]{0,1:T(8,128)S(1)}, ...), condition=%wide.region_7.8_spmd.clone, body=%wide.region_5.7_spmd.clone.sunk | while | flops 883525696 | bytes 9661715 | solution.py:88
  300.9 0.7 dynamic_slice.29
  301.6 1.2 fusion.36
  302.8 2.4 broadcast_multiply_fusion.4
  306.0 4.5 convolution_add_fusion.4
  310.5 0.7 dynamic_slice.31
  313.8 0.7 dynamic_slice.29
  314.5 1.2 fusion.36
  315.7 2.4 broadcast_multiply_fusion.4
  318.9 4.5 convolution_add_fusion.4
  323.4 0.7 dynamic_slice.31
  326.7 0.7 dynamic_slice.29
  327.4 1.2 fusion.36
  328.6 2.4 broadcast_multiply_fusion.4
  331.8 4.5 convolution_add_fusion.4
  336.3 0.7 dynamic_slice.31
  339.6 0.7 dynamic_slice.29
  340.3 1.2 fusion.36
  341.5 2.4 broadcast_multiply_fusion.4
  344.7 4.5 convolution_add_fusion.4
  349.2 0.7 dynamic_slice.31
  352.5 0.7 dynamic_slice.29
  353.2 1.2 fusion.36
  354.4 2.4 broadcast_multiply_fusion.4
  357.6 4.5 convolution_add_fusion.4
  362.1 0.7 dynamic_slice.31
  365.4 0.7 dynamic_slice.29
  366.1 1.2 fusion.36
  367.3 2.4 broadcast_multiply_fusion.4
  370.5 4.5 convolution_add_fusion.4
  375.0 0.7 dynamic_slice.31
  378.3 0.7 dynamic_slice.29
  379.0 1.2 fusion.36
  380.2 2.4 broadcast_multiply_fusion.4
  383.4 4.5 convolution_add_fusion.4
  391.9 1.2 fusion.36
  393.1 2.4 broadcast_multiply_fusion.4
  396.3 4.5 convolution_add_fusion.4
  403.5 1.4 copy.45
  405.7 6.7 %reduce-scatter.10.cloned.1.call-done = f32[32,1]{1,0:T(8,128)} async-done(((f32[64,1]{1,0:T(8,128)}), f32[32,1]{1,0:T(8,128)}) %reduce-scatter.10.cloned.1.call-update) | async-done | bytes 144
  412.4 0.8 copy.44
  413.2 10.1 %reduce-scatter.12.cloned.1.call-done = f32[32,16]{1,0:T(8,128)} async-done(((f32[64,16]{1,0:T(8,128)}), f32[32,16]{1,0:T(8,128)}) %reduce-scatter.12.cloned.1.call-update) | async-done | bytes 2064
  423.3 0.8 copy.46
  424.1 10.7 %reduce-scatter.8.cloned.1.call-done = f32[256,32]{0,1:T(8,128)} async-done(((f32[256,64]{0,1:T(8,128)}), f32[256,32]{0,1:T(8,128)}) %reduce-scatter.8.cloned.1.call-update) | async-done | bytes 32784 | tf_op jit(solution)/shard_map/reduce_scatter | solution.py:91
  434.7 20.1 %all-reduce = (f32[256,32]{0,1:T(8,128)S(1)}, f32[1,32]{1,0:T(1,128)S(1)}, f32[16,32]{1,0:T(8,128)S(1)}) all-reduce(f32[256,32]{0,1:T(8,128)} %reduce-scatter.8.cloned.1.call-done, f32[1,32]{1,0:T(1,128)S(1)} %copy.44, f32[16,32]{1,0:T(8,128)S(1)} %copy.46), channel_id=1, replica_groups=mesh['gx'=4,'gy'=4,'row'=2] {'gy'}, use_global_device_ids=true, to_apply=%region_9.10 | all-reduce | flops 8736 | bytes 69888 | tf_op jit(solution)/shard_map/psum | solution.py:11
  454.8 16.6 %all-reduce.1 = (f32[256,32]{0,1:T(8,128)S(1)}, f32[1,32]{1,0:T(1,128)S(1)}, f32[16,32]{1,0:T(8,128)S(1)}) all-reduce(f32[256,32]{0,1:T(8,128)S(1)} %get-tuple-element.129, f32[1,32]{1,0:T(1,128)S(1)} %get-tuple-element.130, f32[16,32]{1,0:T(8,128)S(1)} %get-tuple-element.131), channel_id=1, replica_groups=mesh['gx'=4,'gy'=4,'row'=2] {'gx'}, use_global_device_ids=true, to_apply=%region_10.11 | all-reduce | flops 8736 | bytes 69888 | tf_op jit(solution)/shard_map/psum | solution.py:12
  472.1 0.8 copy.42
  (106 shorter events, 26.3 us)
Async XLA Ops:
  7.2 99.6 %copy-start = (bf16[137,8192]{1,0:T(8,128)(2,1)S(1)}, bf16[137,8192]{1,0:T(8,128)(2,1)}, u32[]{:S(2)}) copy-start(bf16[137,8192]{1,0:T(8,128)(2,1)} %param.10) | copy-start | bytes 6733828
  67.5 39.3 %copy-start.3 = (bf16[137,16]{0,1:T(8,128)(2,1)S(1)}, bf16[137,16]{0,1:T(8,128)(2,1)}, u32[]{:S(2)}) copy-start(bf16[137,16]{0,1:T(8,128)(2,1)} %param.11) | copy-start | bytes 13156
  98.4 16.0 %all-to-all-start = ((s32[16,1,2048]{2,1,0:T(1,128)}), s32[16,1,2048]{2,1,0:T(1,128)S(1)}, u32[]{:S(2)}, u32[]{:S(2)}) async-start(s32[16,1,2048]{2,1,0:T(1,128)} %bitcast.24), calls=%async_computation | async-start | bytes 262144 | tf_op jit(solution)/shard_map/all_to_all | solution.py:16
  225.8 73.7 %copy-start.2 = (f32[16,32]{1,0:T(8,128)S(1)}, f32[16,32]{1,0:T(8,128)}, u32[]{:S(2)}) copy-start(f32[16,32]{1,0:T(8,128)} %param.12) | copy-start | bytes 6148
  233.6 64.9 %all-to-all-start.1 = ((bf16[16,16,2048]{2,0,1:T(8,128)(2,1)}), bf16[16,16,2048]{2,0,1:T(8,128)(2,1)S(1)}, u32[]{:S(2)}, u32[]{:S(2)}) async-start(bf16[16,16,2048]{2,0,1:T(8,128)(2,1)} %bitcast.13), calls=%async_computation.1 | async-start | bytes 2097152 | tf_op jit(solution)/shard_map/all_to_all | solution.py:20
  237.3 175.1 %reduce-scatter.10.cloned.1.call-start = ((), (), s32[]{:S(2)}) async-start(), calls=%async_computation.6 | async-start | bytes 49152
  299.6 11.7 %copy-start.4 = (f32[16,64]{1,0:T(8,128)S(1)}, f32[16,64]{1,0:T(8,128)}, u32[]{:S(2)}) copy-start(f32[16,64]{1,0:T(8,128)} %get-tuple-element.212) | copy-start | bytes 12292 | tf_op jit(solution)/shard_map/while
  311.8 0.6 copy-start.5
  312.5 11.7 %copy-start.4 = (f32[16,64]{1,0:T(8,128)S(1)}, f32[16,64]{1,0:T(8,128)}, u32[]{:S(2)}) copy-start(f32[16,64]{1,0:T(8,128)} %get-tuple-element.212) | copy-start | bytes 12292 | tf_op jit(solution)/shard_map/while
  324.7 0.6 copy-start.5
  325.4 11.7 %copy-start.4 = (f32[16,64]{1,0:T(8,128)S(1)}, f32[16,64]{1,0:T(8,128)}, u32[]{:S(2)}) copy-start(f32[16,64]{1,0:T(8,128)} %get-tuple-element.212) | copy-start | bytes 12292 | tf_op jit(solution)/shard_map/while
  337.6 0.6 copy-start.5
  338.2 11.7 %copy-start.4 = (f32[16,64]{1,0:T(8,128)S(1)}, f32[16,64]{1,0:T(8,128)}, u32[]{:S(2)}) copy-start(f32[16,64]{1,0:T(8,128)} %get-tuple-element.212) | copy-start | bytes 12292 | tf_op jit(solution)/shard_map/while
  350.5 0.6 copy-start.5
  351.1 11.7 %copy-start.4 = (f32[16,64]{1,0:T(8,128)S(1)}, f32[16,64]{1,0:T(8,128)}, u32[]{:S(2)}) copy-start(f32[16,64]{1,0:T(8,128)} %get-tuple-element.212) | copy-start | bytes 12292 | tf_op jit(solution)/shard_map/while
  363.4 0.6 copy-start.5
  364.1 11.7 %copy-start.4 = (f32[16,64]{1,0:T(8,128)S(1)}, f32[16,64]{1,0:T(8,128)}, u32[]{:S(2)}) copy-start(f32[16,64]{1,0:T(8,128)} %get-tuple-element.212) | copy-start | bytes 12292 | tf_op jit(solution)/shard_map/while
  376.3 0.6 copy-start.5
  376.9 11.7 %copy-start.4 = (f32[16,64]{1,0:T(8,128)S(1)}, f32[16,64]{1,0:T(8,128)}, u32[]{:S(2)}) copy-start(f32[16,64]{1,0:T(8,128)} %get-tuple-element.212) | copy-start | bytes 12292 | tf_op jit(solution)/shard_map/while
  389.2 0.6 copy-start.5
  389.8 11.7 %copy-start.4 = (f32[16,64]{1,0:T(8,128)S(1)}, f32[16,64]{1,0:T(8,128)}, u32[]{:S(2)}) copy-start(f32[16,64]{1,0:T(8,128)} %get-tuple-element.212) | copy-start | bytes 12292 | tf_op jit(solution)/shard_map/while
  402.1 0.6 copy-start.5
  402.7 2.2 copy-start.1
  403.5 19.8 %reduce-scatter.12.cloned.1.call-start = ((), (), s32[]{:S(2)}) async-start(), calls=%async_computation.7 | async-start | bytes 49152
  404.9 29.8 %reduce-scatter.8.cloned.1.call-start = ((), (), s32[]{:S(2)}) async-start(), calls=%async_computation.5 | async-start | bytes 98304 | tf_op jit(solution)/shard_map/reduce_scatter | solution.py:91
Sparse Core Ops, SparseCore 0:
  403.6 8.7 reduce-scatter.9
  414.6 8.6 reduce-scatter.11
  426.0 8.6 reduce-scatter.7
